TPU v7x, 32 devices: a whole 2x2x4 slice. The times are simulated.
32 devices in a mesh: gx: 4 (over y, x), gy: 8 (over z, core).
Axes of the slice: x: 2, y: 2, z: 4, core: 2. Of those that a mesh axis runs over, the one named last changes fastest.
Arguments:
- tiles: bfloat16 [64, 24, 128, 128], P('gx', 'gy'), may hold values from 0.0099487305 to 1
- tile_cols: int32 [64, 24], P('gx', 'gy'), may hold values from 0 to 7
- row_counts: int32 [64, 8], P('gx', 'gy'), may hold values from 0 to 3
- start_block: bfloat16 [8192, 128], P('gx'), may hold values from -6 to 6
Outputs:
- vectors: bfloat16 [8192, 128], P(('gx', 'gy'))
- col_scales: float32 [2, 128], replicated
Inputs may be any that keep to these rules, and one draw needn't show every extreme that they name: `tile_cols`: a column tile inside the slot's block of columns. `row_counts`: slots at or past the count are ignored.
All inputs are finite; a program needn't handle non-finite values.
Results may differ from a plain program's by a relative error of at most 0.0065.
Values may be sent and summed in bfloat16 or wider, within the bound.
A program may use at most 64 MiB of HBM per device.

v0:
```python
import jax
import jax.numpy as jnp
from jax import lax
from jax.sharding import PartitionSpec as P


def on_device(tiles, tile_cols, row_counts, start_block):
    row_tiles = tiles.shape[0]
    slot_count = tiles.shape[1]
    side = tiles.shape[2]
    width = start_block.shape[1]
    groups = lax.axis_size("gx")
    blocks = lax.axis_size("gy")
    col_tiles = row_tiles * groups // blocks
    local_rows = row_tiles * side
    nodes = local_rows * groups
    masks = (jnp.arange(slot_count)[None, :] < row_counts).astype(jnp.bfloat16)
    row_sums = jnp.einsum("rsab,rs->ra", tiles, masks, preferred_element_type=jnp.float32).reshape(
        -1
    )
    degree = 1.0 + lax.psum(row_sums, "gy")
    scale = 1.0 / jnp.sqrt(degree)
    upd = (scale[:, None] * start_block.astype(jnp.float32)).astype(jnp.bfloat16)
    first_tile = lax.axis_index("gy") * col_tiles
    scales = []
    share = local_rows // blocks
    mine = lax.axis_index("gy") * share
    vectors = upd
    for step in range(2):
        whole = lax.all_gather(upd, "gx", axis=0, tiled=True)
        column = lax.dynamic_slice_in_dim(whole, first_tile * side, col_tiles * side, 0)
        product_column = column.reshape(col_tiles, side, width)
        picked = product_column[tile_cols] * masks[:, :, None, None]
        total = jnp.einsum("rsab,rsbk->rak", tiles, picked, preferred_element_type=jnp.float32)
        partial_value = lax.psum(total.reshape(local_rows, width), "gy")
        mixed = scale[:, None] * (partial_value + upd.astype(jnp.float32))
        squares = lax.psum(jnp.sum(mixed * mixed, axis=0), "gx")
        spread = jnp.sqrt(squares / nodes + 1e-06)
        scales.append(spread)
        normed = mixed / spread
        if step == 0:
            upd = (scale[:, None] * normed).astype(jnp.bfloat16)
        else:
            vectors = lax.dynamic_slice_in_dim(normed, mine, share, 0).astype(jnp.bfloat16)
    return (vectors, jnp.stack(scales))


def solution(mesh):
    placed = (P("gx", "gy", None, None), P("gx", "gy"), P("gx", "gy"), P("gx", None))
    return jax.shard_map(
        on_device,
        mesh=mesh,
        in_specs=placed,
        out_specs=(P(("gx", "gy"), None), P()),
        check_vma=False,
    )
```

profile of v0, /device:TPU:0, one launch (start us, length us, event | category | flops | bytes accessed | tf_op | source)
XLA Modules:
  0.0 254.4 jit_solution(1457750543058628907)
XLA Ops:
  7.2 0.0 copy-start.1
  7.2 0.0 all-gather.3.cloned.1.call-start
  7.2 0.8 fusion.9
  8.0 0.0 copy-start.4
  8.0 1.9 convert_reduce_fusion
  9.9 0.1 fusion.7
  10.1 18.4 %psum.35 = f32[2048]{0:T(1024)S(1)} all-reduce(f32[2048]{0:T(1024)S(1)} %bitcast.36), channel_id=1, replica_groups=mesh['gx'=4,'gy'=8] {'gy'}, use_global_device_ids=true, to_apply=%region_1.0 | all-reduce | flops 2048 | bytes 16384 | tf_op jit(solution)/shard_map/psum | solution.py:21
  28.4 0.0 copy-done.1
  28.4 1.1 multiply_convert_fusion.1
  29.6 0.0 all-gather.3.cloned.1.call-update
  29.6 0.0 all-reduce.3.cloned.1.call-start
  29.7 0.0 copy-done.4
  29.7 0.1 copy.7
  29.8 0.1 reshape.52
  29.9 33.3 %all-gather.3.cloned.1.call-done = bf16[8192,128]{1,0:T(8,128)(2,1)} async-done(((bf16[2048,128]{1,0:T(8,128)(2,1)}), bf16[8192,128]{1,0:T(8,128)(2,1)}) %all-gather.3.cloned.1.call-update) | async-done | bytes 2097168 | tf_op jit(solution)/shard_map/all_gather | solution.py:30
  63.1 1.0 constant_dynamic-slice_fusion.1
  64.1 0.0 copy-start
  64.1 0.8 gather_fusion
  65.0 0.5 copy-done
  65.5 1.7 fusion.2
  67.2 0.0 copy-start.2
  67.2 0.0 all-reduce.3.cloned.1.call-update
  67.2 0.0 all-gather.5.cloned.1.call-start
  67.3 59.4 %all-reduce.3.cloned.1.call-done = f32[2048,128]{1,0:T(8,128)} async-done(((f32[2048,128]{1,0:T(8,128)}), f32[2048,128]{1,0:T(8,128)}) %all-reduce.3.cloned.1.call-update) | async-done | bytes 1048592 | tf_op jit(solution)/shard_map/psum | solution.py:35
  126.7 0.0 copy-start.3
  126.7 1.8 multiply_reduce_fusion.1
  128.5 9.8 %psum.37 = f32[128]{0:T(128)S(1)} all-reduce(f32[128]{0:T(128)S(1)} %multiply_reduce_fusion.1), channel_id=1, replica_groups=mesh['gx'=4,'gy'=8] {'gx'}, use_global_device_ids=true, to_apply=%region_4.0 | all-reduce | flops 128 | bytes 1024 | tf_op jit(solution)/shard_map/psum | solution.py:37
  138.3 0.0 copy-done.2
  138.3 0.0 copy-done.3
  138.3 1.1 multiply_convert_fusion
  139.4 0.0 all-gather.5.cloned.1.call-update
  139.5 0.0 all-reduce.5.cloned.1.call-start
  139.5 32.7 %all-gather.5.cloned.1.call-done = bf16[8192,128]{1,0:T(8,128)(2,1)} async-done(((bf16[2048,128]{1,0:T(8,128)(2,1)}), bf16[8192,128]{1,0:T(8,128)(2,1)}) %all-gather.5.cloned.1.call-update) | async-done | bytes 2097168 | tf_op jit(solution)/shard_map/all_gather | solution.py:30
  172.2 1.0 constant_dynamic-slice_fusion
  173.1 0.8 gather_fusion.1
  174.0 1.7 fusion
  175.7 0.0 all-reduce.5.cloned.1.call-update
  175.7 59.4 %all-reduce.5.cloned.1.call-done = f32[2048,128]{1,0:T(8,128)} async-done(((f32[2048,128]{1,0:T(8,128)}), f32[2048,128]{1,0:T(8,128)}) %all-reduce.5.cloned.1.call-update) | async-done | bytes 1048592 | tf_op jit(solution)/shard_map/psum | solution.py:35
  235.1 1.7 multiply_reduce_fusion
  236.8 9.8 %psum.39 = f32[128]{0:T(128)S(1)} all-reduce(f32[128]{0:T(128)S(1)} %get-tuple-element.2), channel_id=1, replica_groups=mesh['gx'=4,'gy'=8] {'gx'}, use_global_device_ids=true, to_apply=%region_7.0 | all-reduce | flops 128 | bytes 1024 | tf_op jit(solution)/shard_map/psum | solution.py:37
  246.6 0.6 pad_maximum_fusion
  247.2 0.6 fusion.6
  (5 shorter events, 0.0 us)
Async XLA Ops:
  7.2 21.3 %copy-start.1 = (bf16[2048,128]{1,0:T(8,128)(2,1)S(1)}, bf16[2048,128]{1,0:T(8,128)(2,1)}, u32[]{:S(2)}) copy-start(bf16[2048,128]{1,0:T(8,128)(2,1)} %param.7) | copy-start | bytes 1572868
  7.2 56.0 %all-gather.3.cloned.1.call-start = ((), (), s32[]{:S(2)}) async-start(), calls=%async_computation | async-start | bytes 2621440 | tf_op jit(solution)/shard_map/all_gather | solution.py:30
  8.0 21.7 %copy-start.4 = (s32[16,3]{0,1:T(4,128)S(1)}, s32[16,3]{0,1:T(4,128)}, u32[]{:S(2)}) copy-start(s32[16,3]{0,1:T(4,128)} %param.5) | copy-start | bytes 580
  29.6 97.1 %all-reduce.3.cloned.1.call-start = ((), (), s32[]{:S(2)}) async-start(), calls=%async_computation.1 | async-start | bytes 2097152 | tf_op jit(solution)/shard_map/psum | solution.py:35
  64.1 1.4 copy-start
  67.2 71.1 %copy-start.2 = (bf16[2048,128]{1,0:T(8,128)(2,1)S(1)}, bf16[2048,128]{1,0:T(8,128)(2,1)}, u32[]{:S(2)}) copy-start(bf16[2048,128]{1,0:T(8,128)(2,1)} %param.7) | copy-start | bytes 1572868
  67.2 104.9 %all-gather.5.cloned.1.call-start = ((), (), s32[]{:S(2)}) async-start(), calls=%async_computation.2 | async-start | bytes 2621440 | tf_op jit(solution)/shard_map/all_gather | solution.py:30
  126.7 11.6 %copy-start.3 = (f32[2048,128]{1,0:T(8,128)S(1)}, f32[2048,128]{1,0:T(8,128)}, u32[]{:S(2)}) copy-start(f32[2048,128]{1,0:T(8,128)} %all-reduce.3.cloned.1.call-done) | copy-start | bytes 3145732
  139.5 95.6 %all-reduce.5.cloned.1.call-start = ((), (), s32[]{:S(2)}) async-start(), calls=%async_computation.3 | async-start | bytes 2097152 | tf_op jit(solution)/shard_map/psum | solution.py:35
Sparse Core Ops, SparseCore 0:
  29.7 33.3 all-gather.2
  67.4 59.2 all-reduce.2
  139.6 32.5 all-gather.4
  175.8 59.2 all-reduce.4
where the time goes:
time: 255 us; the launch traced here: 254 us
  waiting for transfers between devices  185 us (73%)
  blocking collectives  37.9 us (15%)
  between operations  13.9 us (5%)
  other arithmetic  9.73 us (4%)
  local copies, waits for them, and re-layouts  4.37 us (2%)
  matrix products  3.51 us (1%)
    psum x2, waiting for transfers between devices, on_device(): partial_value = lax.psum(total.reshape(local_rows, width), 'gy')  119 us
    all_gather x2, waiting for transfers between devices, on_device(): whole = lax.all_gather(upd, 'gx', axis=0, tiled=True)  65.9 us
    psum x2, blocking collectives, on_device(): squares = lax.psum(jnp.sum(mixed * mixed, axis=0), 'gx')  19.6 us
    psum x1, blocking collectives, on_device(): degree = 1.0 + lax.psum(row_sums, 'gy')  18.4 us
  transfers between devices with their start and end apart: 4, of which 4 were waited for; matrix products, arithmetic and copies ran while one was open for 0% of the time, Pallas kernels for 0%

commit v1 on v0

v1 whole, which is shorter than its diff:
```python
import functools
import jax
import jax.numpy as jnp
from jax import lax
from jax.experimental import pallas as pl
from jax.experimental.pallas import tpu as pltpu
from jax.sharding import PartitionSpec as P

MESH = pl.DeviceIdType.MESH
LOADS = 4


def wait(ref, sem):
    pltpu.make_async_copy(ref, ref, sem).wait()


def kernel(
    groups,
    blocks,
    tiles_hbm,
    start_hbm,
    cols,
    counts,
    out,
    sums_out,
    tiles,
    sbuf,
    ubuf,
    vbuf,
    scol,
    sshare,
    rs,
    deg_col,
    deg_share,
    psend,
    precv,
    acc,
    csend,
    clow,
    chigh,
    p2send,
    p2recv,
    r2send,
    r2recv,
    last,
    sq,
    tsem,
    ssend,
    srecv,
    dcs,
    dcr,
    dss,
    dsr,
    psd,
    prc,
    csd,
    clr,
    chr_,
    vsend,
    vrecv,
    p2s,
    p2r,
    r2s,
    r2r,
    qs,
    qr,
):
    row_tiles, slots, side, _ = tiles.shape
    width = acc.shape[1]
    depth = acc.shape[0]
    col_tiles = depth // side
    share = out.shape[0]
    floors = blocks // 2
    total = groups * blocks
    nodes = groups * row_tiles * side
    piece = min(side, share)
    pieces = share // piece
    share_tiles = max(1, share // side)
    square = groups == 4

    i = lax.axis_index("gx")
    j = lax.axis_index("gy")
    z = lax.div(j, 2)
    c = lax.rem(j, 2)
    me = i * blocks + j
    root = i == z
    if square:
        x, y = lax.rem(i, 2), lax.div(i, 2)
        across_x = y * 2 + 1 - x
        across_y = (1 - y) * 2 + x
        off_x = x != lax.rem(z, 2)
        off_y = y != lax.div(z, 2)
        only_x = jnp.logical_and(off_x, jnp.logical_not(off_y))
        only_y = jnp.logical_and(off_y, jnp.logical_not(off_x))
        fan = 2
    else:
        fan = groups - 1

    def rows(ref, t):
        if len(ref.shape) == 3:
            return ref.at[t]
        return ref.at[pl.ds(t * side, side)]

    def remote(src, dst, send, recv, gx, gy):
        return pltpu.make_async_remote_copy(
            src_ref=src,
            dst_ref=dst,
            send_sem=send,
            recv_sem=recv,
            device_id=(gx, gy),
            device_id_type=MESH,
        )

    def fan_out(buf, send, recv, t):
        for p in range(fan):
            if square:
                target = (across_x, across_y)[p]
            else:
                target = lax.rem(i + p + 1, groups)
            remote(rows(buf, t), rows(buf, t), send.at[p, t], recv.at[t], target, j).start()

    def pass_on(buf, send, recv, t):
        if square:
            cond, target = ((only_x, across_y), (only_y, across_x))[t % 2]

            @pl.when(cond)
            def _():
                remote(rows(buf, t), rows(buf, t), send.at[0, t], recv.at[t], target, j).start()

    def fan_done(buf, send):
        @pl.when(root)
        def _():
            for t in range(col_tiles):
                for p in range(fan):
                    wait(rows(buf, t), send.at[p, t])

        if square:
            for parity, cond in ((0, only_x), (1, only_y)):

                @pl.when(cond)
                def _():
                    for t in range(parity, col_tiles, 2):
                        wait(rows(buf, t), send.at[0, t])

    step = row_tiles // LOADS
    loads = [
        pltpu.make_async_copy(
            tiles_hbm.at[pl.ds(n * step, step)], tiles.at[pl.ds(n * step, step)], tsem.at[n]
        )
        for n in range(LOADS)
    ]
    barrier = pltpu.get_barrier_semaphore()

    @pl.loop(1, total)
    def _(k):
        other = lax.rem(me + k, total)
        pl.semaphore_signal(
            barrier,
            inc=1,
            device_id=(lax.div(other, blocks), lax.rem(other, blocks)),
            device_id_type=MESH,
        )

    @pl.when(root)
    def _():
        for t in range(col_tiles):
            pltpu.make_async_copy(
                start_hbm.at[pl.ds(c * depth + t * side, side)], rows(sbuf, t), srecv.at[t]
            ).start()

    for load in loads:
        load.start()
    ubuf[col_tiles] = jnp.zeros((side, width), ubuf.dtype)
    vbuf[col_tiles] = jnp.zeros((side, width), vbuf.dtype)
    pl.semaphore_wait(barrier, total - 1)

    @pl.when(root)
    def _():
        for t in range(col_tiles):
            wait(rows(sbuf, t), srecv.at[t])
            fan_out(sbuf, ssend, srecv, t)

    ones = jnp.ones((8, side), jnp.bfloat16)
    for r in range(row_tiles):
        if r % step == 0:
            loads[r // step].wait()
        count = counts[r, 0]
        row = jnp.zeros((8, side), jnp.float32)
        for s in range(slots):
            part = lax.dot_general(
                ones, tiles[r, s], (((1,), (1,)), ((), ())), preferred_element_type=jnp.float32
            )
            row = row + jnp.clip(count - s, 0, 1).astype(jnp.float32) * part
        rs[r] = row[0:1]

    for h in range(2):
        source = rs.at[pl.ds(h * col_tiles, col_tiles)]
        for n in range(groups):
            target = lax.rem(i + n, groups)
            gy = 2 * i + h
            slot = deg_col.at[j]
            mine = jnp.logical_and(n == 0, gy == j)

            @pl.when(jnp.logical_not(mine))
            def _():
                remote(source, slot, dcs.at[h * groups + n], dcr.at[j], target, gy).start()

            @pl.when(mine)
            def _():
                pltpu.make_async_copy(source, slot, dcr.at[j]).start()

    def share_of(gy):
        return rs.at[pl.ds(lax.div(gy * share, side), share_tiles)]

    for n in range(1, blocks):
        gy = lax.rem(j + n, blocks)
        remote(share_of(gy), deg_share.at[j], dss.at[n], dsr.at[j], i, gy).start()
    pltpu.make_async_copy(share_of(j), deg_share.at[j], dsr.at[j]).start()

    @pl.when(jnp.logical_not(root))
    def _():
        for t in range(col_tiles):
            wait(rows(sbuf, t), srecv.at[t])
            pass_on(sbuf, ssend, srecv, t)

    for n in range(blocks):
        wait(deg_col.at[n], dcr.at[n])

    def upright(degree):
        scale = 1.0 / jnp.sqrt(1.0 + degree)
        return jnp.transpose(jnp.broadcast_to(scale, (side, side)))

    for t in range(col_tiles):
        degree = deg_col[0, t]
        for n in range(1, blocks):
            degree = degree + deg_col[n, t]
        scale = upright(degree)[:, :1]
        scale = jnp.broadcast_to(scale, (side, width))
        scol[pl.ds(t * side, side)] = scale
        ubuf[t] = (scale * sbuf[t].astype(jnp.float32)).astype(ubuf.dtype)

    def product(buf, r, off, height):
        count = counts[r, 0]
        value = None
        for s in range(slots):
            live = jnp.clip(count - s, 0, 1)
            block = buf[live * cols[r, s] + (1 - live) * col_tiles]
            left = tiles[r, s] if height == side else tiles[r, s, pl.ds(off, height)]
            term = jnp.dot(left, block, preferred_element_type=jnp.float32)
            value = term if value is None else value + term
        return value

    for t in range(col_tiles):
        psend[pl.ds(t * side, side)] = product(ubuf, (1 - c) * col_tiles + t, 0, side).astype(
            psend.dtype
        )
        remote(rows(psend, t), rows(precv, t), psd.at[t], prc.at[t], i, j + 1 - 2 * c).start()

    below = jnp.logical_and(z > 0, z <= i)
    above = jnp.logical_and(z < floors - 1, z >= i)
    sq[0] = jnp.zeros_like(sq[0])
    for t in range(col_tiles):
        acc[pl.ds(t * side, side)] = product(ubuf, c * col_tiles + t, 0, side)
    for t in range(col_tiles):
        here = pl.ds(t * side, side)
        wait(rows(precv, t), prc.at[t])
        acc[here] += precv[here].astype(jnp.float32)

        @pl.when(below)
        def _():
            wait(rows(clow, t), clr.at[t])
            acc[here] += clow[here].astype(jnp.float32)

        @pl.when(above)
        def _():
            wait(rows(chigh, t), chr_.at[t])
            acc[here] += chigh[here].astype(jnp.float32)

        @pl.when(jnp.logical_not(root))
        def _():
            csend[here] = acc[here].astype(csend.dtype)

        @pl.when(z < i)
        def _():
            remote(rows(csend, t), rows(clow, t), csd.at[t], clr.at[t], i, j + 2).start()

        @pl.when(z > i)
        def _():
            remote(rows(csend, t), rows(chigh, t), csd.at[t], chr_.at[t], i, j - 2).start()

        @pl.when(root)
        def _():
            mixed = scol[here] * (acc[here] + ubuf[t].astype(jnp.float32))
            vbuf[t] = (scol[here] * mixed).astype(vbuf.dtype)
            fan_out(vbuf, vsend, vrecv, t)
            sq[0, 0:1] += jnp.sum(mixed * mixed, axis=0, keepdims=True)

    for n in range(blocks):
        wait(deg_share.at[n], dsr.at[n])
    for t in range(share_tiles):
        degree = deg_share[0, t]
        for n in range(1, blocks):
            degree = degree + deg_share[n, t]
        sshare[pl.ds(t * side, side)] = jnp.broadcast_to(upright(degree)[:, :1], (side, width))

    @pl.when(jnp.logical_not(root))
    def _():
        for t in range(col_tiles):
            wait(rows(vbuf, t), vrecv.at[t])
            pass_on(vbuf, vsend, vrecv, t)

    def share_product(gy, put):
        for p in range(pieces):
            first = gy * share + p * piece
            off = pl.multiple_of(lax.rem(first, side), piece) if piece < side else 0
            value = product(vbuf, lax.div(first, side), off, piece)
            own = jnp.logical_and(root, lax.div(first, depth) == c)
            tile = lax.div(lax.rem(first, depth), side)
            block = vbuf[tile] if piece == side else vbuf[tile, pl.ds(off, piece)]
            put(p, value + jnp.where(own, block.astype(jnp.float32), 0.0))

    for n in range(1, floors + 1):
        floor = lax.rem(z + n, floors)

        def put(p, value):
            p2send[floor, pl.ds(p * piece, piece)] = value.astype(p2send.dtype)

        share_product(2 * floor + 1 - c, put)
        remote(
            p2send.at[floor], p2recv.at[floor], p2s.at[floor], p2r.at[floor], i, j + 1 - 2 * c
        ).start()

    for n in range(1, floors + 1):
        floor = lax.rem(z + n, floors)

        def put(p, value):
            last[pl.ds(p * piece, piece)] = value

        share_product(2 * floor + c, put)
        wait(p2recv.at[floor], p2r.at[floor])
        last[...] += p2recv[floor].astype(jnp.float32)
        if n < floors:
            r2send[floor] = last[...].astype(r2send.dtype)
            remote(
                r2send.at[floor], r2recv.at[z], r2s.at[floor], r2r.at[z], i, 2 * floor + c
            ).start()

    for n in range(1, floors):
        floor = lax.rem(z + n, floors)
        wait(r2recv.at[floor], r2r.at[floor])
        last[...] += r2recv[floor].astype(jnp.float32)

    if share < side:
        begin = pl.multiple_of(lax.rem(j * share, side), share)
        mixed = sshare[pl.ds(begin, share)] * last[...]
    else:
        mixed = sshare[...] * last[...]
    last[...] = mixed
    sq[0, 1:2] = jnp.sum(mixed * mixed, axis=0, keepdims=True)

    @pl.loop(1, total)
    def _(k):
        other = lax.rem(me + k, total)
        remote(
            sq.at[0],
            sq.at[total - k],
            qs,
            qr,
            lax.div(other, blocks),
            lax.rem(other, blocks),
        ).start()

    fan_done(sbuf, ssend)
    fan_done(vbuf, vsend)
    for h in range(2):
        source = rs.at[pl.ds(h * col_tiles, col_tiles)]
        for n in range(groups):
            if n > 0:
                wait(source, dcs.at[h * groups + n])
            else:

                @pl.when(2 * i + h != j)
                def _():
                    wait(source, dcs.at[h * groups + n])

    for n in range(1, blocks):
        wait(share_of(j), dss.at[n])
    for t in range(col_tiles):
        wait(rows(psend, t), psd.at[t])

    @pl.when(jnp.logical_not(root))
    def _():
        for t in range(col_tiles):
            wait(rows(csend, t), csd.at[t])

    for n in range(1, floors + 1):
        floor = lax.rem(z + n, floors)
        wait(p2send.at[floor], p2s.at[floor])
        if n < floors:
            wait(r2send.at[floor], r2s.at[floor])

    others = sq.at[pl.ds(1, total - 1)]
    wait(others, qs)
    wait(others, qr)
    sums = jnp.sum(sq[...], axis=0)
    first = jnp.sqrt(sums[0:1] / nodes + 1e-06)
    second = jnp.sqrt(sums[1:2] / (first * first) / nodes + 1e-06)
    sums_out[0:1] = first
    sums_out[1:2] = second
    out[...] = last[...] / (first * second)


def on_device(groups, blocks, tiles, tile_cols, row_counts, start_block):
    row_tiles, slots, side, _ = tiles.shape
    width = start_block.shape[1]
    local_rows = row_tiles * side
    depth = local_rows * groups // blocks
    col_tiles = depth // side
    share = local_rows // blocks
    share_tiles = max(1, share // side)
    floors = blocks // 2
    total = groups * blocks
    fan = 2 if groups == 4 else groups - 1
    bf16, f32 = jnp.bfloat16, jnp.float32
    vmem, dma = pltpu.VMEM, pltpu.SemaphoreType.DMA
    spec = pl.BlockSpec
    out, scales = pl.pallas_call(
        functools.partial(kernel, groups, blocks),
        out_shape=(
            jax.ShapeDtypeStruct((share, width), f32),
            jax.ShapeDtypeStruct((2, width), f32),
        ),
        in_specs=[
            spec(memory_space=pl.ANY),
            spec(memory_space=pl.ANY),
            spec(memory_space=pltpu.SMEM),
            spec(memory_space=pltpu.SMEM),
        ],
        out_specs=(spec(memory_space=pltpu.VMEM), spec(memory_space=pltpu.VMEM)),
        scratch_shapes=[
            vmem(tiles.shape, bf16),
            vmem((col_tiles, side, width), bf16),
            vmem((col_tiles + 1, side, width), bf16),
            vmem((col_tiles + 1, side, width), bf16),
            vmem((depth, width), f32),
            vmem((share_tiles * side, width), f32),
            vmem((row_tiles, 1, side), f32),
            vmem((blocks, col_tiles, 1, side), f32),
            vmem((blocks, share_tiles, 1, side), f32),
            vmem((depth, width), bf16),
            vmem((depth, width), bf16),
            vmem((depth, width), f32),
            vmem((depth, width), bf16),
            vmem((depth, width), bf16),
            vmem((depth, width), bf16),
            vmem((floors, share, width), bf16),
            vmem((floors, share, width), bf16),
            vmem((floors, share, width), bf16),
            vmem((floors, share, width), bf16),
            vmem((share, width), f32),
            vmem((total, 2, width), f32),
            dma((LOADS,)),
            dma((fan, col_tiles)),
            dma((col_tiles,)),
            dma((2 * groups,)),
            dma((blocks,)),
            dma((blocks,)),
            dma((blocks,)),
            dma((col_tiles,)),
            dma((col_tiles,)),
            dma((col_tiles,)),
            dma((col_tiles,)),
            dma((col_tiles,)),
            dma((fan, col_tiles)),
            dma((col_tiles,)),
            dma((floors,)),
            dma((floors,)),
            dma((floors,)),
            dma((floors,)),
            dma,
            dma,
        ],
        compiler_params=pltpu.CompilerParams(collective_id=0, has_side_effects=True),
    )(tiles, start_block, tile_cols, row_counts)
    return out.astype(bf16), scales


def solution(mesh):
    placed = (P("gx", "gy", None, None), P("gx", "gy"), P("gx", "gy"), P("gx", None))
    return jax.shard_map(
        functools.partial(on_device, mesh.shape["gx"], mesh.shape["gy"]),
        mesh=mesh,
        in_specs=placed,
        out_specs=(P(("gx", "gy"), None), P()),
        check_vma=False,
    )
```

time: 255 us -> 60 us (0.24)
  waiting for transfers between devices: 185 us -> 0 us
  Pallas kernels: 0 us -> 53.6 us
  blocking collectives: 37.9 us -> 0 us
  between operations: 13.9 us -> 0.64 us
  other arithmetic: 9.73 us -> 1.54 us
  matrix products: 3.51 us -> 0 us
    psum x2 -> x0, waiting for transfers between devices: 119 us -> none  [on_device(): partial_value = lax.psum(total.reshape(local_rows, width), 'gy')]
    all_gather x2 -> x0, waiting for transfers between devices: 65.9 us -> none  [on_device(): whole = lax.all_gather(upd, 'gx', axis=0, tiled=True)]
    pallas_call x0 -> x1, Pallas kernels: none -> 53.6 us  [on_device(): pl.pallas_call(functools.partial(kernel, groups, blocks), out_shape=(jax....]
    psum x3 -> x0, blocking collectives: 37.9 us -> none  [the longest x2 19.6 us: on_device(): squares = lax.psum(jnp.sum(mixed * mixed, axis=0), 'gx')]
    reduce_sum x3 -> x0, other arithmetic: 5.42 us -> none  [the longest x2 3.5 us: on_device(): squares = lax.psum(jnp.sum(mixed * mixed, axis=0), 'gx')]
    dot_general x3 -> x0, matrix products: 3.51 us -> none  [the longest x2 3.37 us: on_device(): jnp.einsum('rsab,rsbk->rak', tiles, picked, preferred_element_type=jnp.fl...]
    unnamed x10 -> x3, local copies, waits for them, and re-layouts: 0.56 us -> 3.9 us
  transfers between devices with their start and end apart: 4 -> 0, of which waited for: 4 -> 0; matrix products, arithmetic and copies ran while one was open for 0% -> 0% of each run, Pallas kernels for 0% -> 0%
where the time goes in v1:
time: 60 us; the launch traced here: 59.7 us
  Pallas kernels  53.6 us (89%)
  local copies, waits for them, and re-layouts  3.9 us (6%)
  other arithmetic  1.54 us (3%)
  between operations  0.64 us (1%)
    pallas_call x1, Pallas kernels, on_device(): pl.pallas_call(functools.partial(kernel, groups, blocks), out_shape=(jax....  53.6 us
    unnamed x3, local copies, waits for them, and re-layouts  3.9 us
    convert_element_type x1, other arithmetic, on_device(): return (out.astype(bf16), scales)  1.54 us

profile of v1, /device:TPU:0, one launch (start us, length us, event | category | flops | bytes accessed | tf_op | source)
XLA Modules:
  0.0 59.7 jit_solution(2562675012476417659)
XLA Ops:
  0.6 1.4 %copy.6.cols = s32[16,3]{1,0:T(8,128)} copy(s32[16,3]{0,1:T(4,128)} %param.5) | data formatting | bytes 384 | tf_op args[1]
  2.0 1.3 %copy.7.counts = s32[16,1]{1,0:T(8,128)} copy(s32[16,1]{0,1:T(1,128)} %param.6) | data formatting | bytes 128 | tf_op args[2]
  3.3 53.6 %shard_map.59 = (f32[256,128]{1,0:T(8,128)}, f32[2,128]{1,0:T(2,128)}) custom-call(bf16[16,3,128,128]{3,2,1,0:T(8,128)(2,1)} %tiles_hbm.1, bf16[2048,128]{1,0:T(8,128)(2,1)} %start_hbm.1, s32[16,3]{1,0:T(8,128)} %copy.6.cols, s32[16,1]{1,0:T(8,128)} %copy.7.counts), custom_call_target="tpu_custom_call" | custom-call | tf_op jit(solution)/shard_map/pallas_call | solution.py:427
  56.9 1.5 %convert_element_type.3 = bf16[256,128]{1,0:T(8,128)(2,1)} convert(f32[256,128]{1,0:T(8,128)} %get-tuple-element.4) | non-fusion elementwise | flops 32768 | bytes 196608 | tf_op jit(solution)/shard_map/convert_element_type | solution.py:485
  58.5 1.2 %copy.9 = f32[2,128]{1,0:T(2,128)} copy(f32[2,128]{1,0:T(2,128)} %get-tuple-element.9) | data formatting | bytes 2048

commit v2 on v1

--- a/solution.py
+++ b/solution.py
@@ -8,6 +8,8 @@
 
 MESH = pl.DeviceIdType.MESH
 LOADS = 4
+LAG = 4
+LAG2 = 1
 
 
 def wait(ref, sem):
@@ -64,15 +66,14 @@
     r2r,
     qs,
     qr,
+    gate,
 ):
     row_tiles, slots, side, _ = tiles.shape
-    width = acc.shape[1]
-    depth = acc.shape[0]
-    col_tiles = depth // side
+    col_tiles, _, width = acc.shape
+    depth = col_tiles * side
     share = out.shape[0]
     floors = blocks // 2
     total = groups * blocks
-    nodes = groups * row_tiles * side
     piece = min(side, share)
     pieces = share // piece
     share_tiles = max(1, share // side)
@@ -93,8 +94,12 @@
         only_x = jnp.logical_and(off_x, jnp.logical_not(off_y))
         only_y = jnp.logical_and(off_y, jnp.logical_not(off_x))
         fan = 2
+        halves = 2
     else:
         fan = groups - 1
+        halves = 1
+    chunks = col_tiles * halves
+    height_of = side // halves
 
     def rows(ref, t):
         if len(ref.shape) == 3:
@@ -111,15 +116,18 @@
             device_id_type=MESH,
         )
 
-    def fan_out(buf, send, recv, t):
-        for p in range(fan):
+    def bit(ref, t):
+        return ref.at[t // halves, pl.ds(t % halves * height_of, height_of)]
+
+    def fan_out(buf, send, recv, t, rows, only=None):
+        for p in range(fan) if only is None else (only,):
             if square:
                 target = (across_x, across_y)[p]
             else:
                 target = lax.rem(i + p + 1, groups)
             remote(rows(buf, t), rows(buf, t), send.at[p, t], recv.at[t], target, j).start()
 
-    def pass_on(buf, send, recv, t):
+    def pass_on(buf, send, recv, t, rows):
         if square:
             cond, target = ((only_x, across_y), (only_y, across_x))[t % 2]
 
@@ -127,10 +135,12 @@
             def _():
                 remote(rows(buf, t), rows(buf, t), send.at[0, t], recv.at[t], target, j).start()
 
-    def fan_done(buf, send):
+    def fan_done(buf, send, rows):
+        amount = send.shape[1]
+
         @pl.when(root)
         def _():
-            for t in range(col_tiles):
+            for t in range(amount):
                 for p in range(fan):
                     wait(rows(buf, t), send.at[p, t])
 
@@ -139,7 +149,7 @@
 
                 @pl.when(cond)
                 def _():
-                    for t in range(parity, col_tiles, 2):
+                    for t in range(parity, amount, 2):
                         wait(rows(buf, t), send.at[0, t])
 
     step = row_tiles // LOADS
@@ -151,15 +161,13 @@
     ]
     barrier = pltpu.get_barrier_semaphore()
 
-    @pl.loop(1, total)
-    def _(k):
-        other = lax.rem(me + k, total)
-        pl.semaphore_signal(
-            barrier,
-            inc=1,
-            device_id=(lax.div(other, blocks), lax.rem(other, blocks)),
-            device_id_type=MESH,
-        )
+    def greet(semaphore, gx, gy):
+        pl.semaphore_signal(semaphore, inc=1, device_id=(gx, gy), device_id_type=MESH)
+
+    for n in range(1, groups):
+        greet(barrier, lax.rem(i + n, groups), j)
+    for n in range(1, blocks):
+        greet(barrier, i, lax.rem(j + n, blocks))
 
     @pl.when(root)
     def _():
@@ -172,19 +180,28 @@
         load.start()
     ubuf[col_tiles] = jnp.zeros((side, width), ubuf.dtype)
     vbuf[col_tiles] = jnp.zeros((side, width), vbuf.dtype)
-    pl.semaphore_wait(barrier, total - 1)
+    pl.semaphore_wait(barrier, groups + blocks - 2)
+    for n in range(1, groups):
+        greet(gate, lax.rem(i + n, groups), j)
 
     @pl.when(root)
     def _():
         for t in range(col_tiles):
             wait(rows(sbuf, t), srecv.at[t])
-            fan_out(sbuf, ssend, srecv, t)
+        if square:
+            for turn in range(2):
+                for t in range(0, col_tiles, 2):
+                    fan_out(sbuf, ssend, srecv, t + turn, rows, 0)
+                    fan_out(sbuf, ssend, srecv, t + 1 - turn, rows, 1)
+        else:
+            for t in range(col_tiles):
+                fan_out(sbuf, ssend, srecv, t, rows)
 
     ones = jnp.ones((8, side), jnp.bfloat16)
     for r in range(row_tiles):
         if r % step == 0:
             loads[r // step].wait()
-        count = counts[r, 0]
+        count = counts[0, r]
         row = jnp.zeros((8, side), jnp.float32)
         for s in range(slots):
             part = lax.dot_general(
@@ -193,6 +210,7 @@
             row = row + jnp.clip(count - s, 0, 1).astype(jnp.float32) * part
         rs[r] = row[0:1]
 
+    pl.semaphore_wait(gate, groups - 1)
     for h in range(2):
         source = rs.at[pl.ds(h * col_tiles, col_tiles)]
         for n in range(groups):
@@ -217,11 +235,14 @@
         remote(share_of(gy), deg_share.at[j], dss.at[n], dsr.at[j], i, gy).start()
     pltpu.make_async_copy(share_of(j), deg_share.at[j], dsr.at[j]).start()
 
-    @pl.when(jnp.logical_not(root))
-    def _():
-        for t in range(col_tiles):
-            wait(rows(sbuf, t), srecv.at[t])
-            pass_on(sbuf, ssend, srecv, t)
+    if square:
+        for parity, cond in ((0, only_x), (1, only_y)):
+
+            @pl.when(cond)
+            def _():
+                for t in range(parity, col_tiles, 2):
+                    wait(rows(sbuf, t), srecv.at[t])
+                    pass_on(sbuf, ssend, srecv, t, rows)
 
     for n in range(blocks):
         wait(deg_col.at[n], dcr.at[n])
@@ -235,45 +256,57 @@
         for n in range(1, blocks):
             degree = degree + deg_col[n, t]
         scale = upright(degree)[:, :1]
-        scale = jnp.broadcast_to(scale, (side, width))
-        scol[pl.ds(t * side, side)] = scale
-        ubuf[t] = (scale * sbuf[t].astype(jnp.float32)).astype(ubuf.dtype)
+        scol[t] = jnp.broadcast_to(scale, (side, width))
+
+    for t in range(col_tiles):
+        if square:
+            done = jnp.logical_or(root, (only_x, only_y)[t % 2])
+        else:
+            done = root
+
+        @pl.when(jnp.logical_not(done))
+        def _():
+            wait(rows(sbuf, t), srecv.at[t])
+
+    for t in range(col_tiles):
+        ubuf[t] = (scol[t] * sbuf[t].astype(jnp.float32)).astype(ubuf.dtype)
 
     def product(buf, r, off, height):
-        count = counts[r, 0]
+        count = counts[0, r]
         value = None
         for s in range(slots):
             live = jnp.clip(count - s, 0, 1)
-            block = buf[live * cols[r, s] + (1 - live) * col_tiles]
+            block = buf[live * cols[s, r] + (1 - live) * col_tiles]
             left = tiles[r, s] if height == side else tiles[r, s, pl.ds(off, height)]
             term = jnp.dot(left, block, preferred_element_type=jnp.float32)
             value = term if value is None else value + term
         return value
 
-    for t in range(col_tiles):
-        psend[pl.ds(t * side, side)] = product(ubuf, (1 - c) * col_tiles + t, 0, side).astype(
-            psend.dtype
-        )
-        remote(rows(psend, t), rows(precv, t), psd.at[t], prc.at[t], i, j + 1 - 2 * c).start()
-
     below = jnp.logical_and(z > 0, z <= i)
     above = jnp.logical_and(z < floors - 1, z >= i)
     sq[0] = jnp.zeros_like(sq[0])
-    for t in range(col_tiles):
-        acc[pl.ds(t * side, side)] = product(ubuf, c * col_tiles + t, 0, side)
-    for t in range(col_tiles):
-        here = pl.ds(t * side, side)
+
+    def give(t):
+        psend[t] = product(ubuf, (1 - c) * col_tiles + t, 0, side).astype(psend.dtype)
+        remote(rows(psend, t), rows(precv, t), psd.at[t], prc.at[t], i, j + 1 - 2 * c).start()
+
+    def combine(t):
         wait(rows(precv, t), prc.at[t])
-        acc[here] += precv[here].astype(jnp.float32)
+        acc[t] += precv[t].astype(jnp.float32)
+        for u in range(t * halves, (t + 1) * halves):
+            advance(u)
+
+    def advance(u):
+        here = (u // halves, pl.ds(u % halves * height_of, height_of))
 
         @pl.when(below)
         def _():
-            wait(rows(clow, t), clr.at[t])
+            wait(bit(clow, u), clr.at[u])
             acc[here] += clow[here].astype(jnp.float32)
 
         @pl.when(above)
         def _():
-            wait(rows(chigh, t), chr_.at[t])
+            wait(bit(chigh, u), chr_.at[u])
             acc[here] += chigh[here].astype(jnp.float32)
 
         @pl.when(jnp.logical_not(root))
@@ -282,18 +315,25 @@
 
         @pl.when(z < i)
         def _():
-            remote(rows(csend, t), rows(clow, t), csd.at[t], clr.at[t], i, j + 2).start()
+            remote(bit(csend, u), bit(clow, u), csd.at[u], clr.at[u], i, j + 2).start()
 
         @pl.when(z > i)
         def _():
-            remote(rows(csend, t), rows(chigh, t), csd.at[t], chr_.at[t], i, j - 2).start()
+            remote(bit(csend, u), bit(chigh, u), csd.at[u], chr_.at[u], i, j - 2).start()
 
         @pl.when(root)
         def _():
-            mixed = scol[here] * (acc[here] + ubuf[t].astype(jnp.float32))
-            vbuf[t] = (scol[here] * mixed).astype(vbuf.dtype)
-            fan_out(vbuf, vsend, vrecv, t)
+            mixed = scol[here] * (acc[here] + ubuf[here].astype(jnp.float32))
+            vbuf[here] = (scol[here] * mixed).astype(vbuf.dtype)
+            fan_out(vbuf, vsend, vrecv, u, bit)
             sq[0, 0:1] += jnp.sum(mixed * mixed, axis=0, keepdims=True)
+
+    for t in range(col_tiles + LAG):
+        if t < col_tiles:
+            give(t)
+        if t >= LAG:
+            acc[t - LAG] = product(ubuf, c * col_tiles + t - LAG, 0, side)
+            combine(t - LAG)
 
     for n in range(blocks):
         wait(deg_share.at[n], dsr.at[n])
@@ -305,9 +345,9 @@
 
     @pl.when(jnp.logical_not(root))
     def _():
-        for t in range(col_tiles):
-            wait(rows(vbuf, t), vrecv.at[t])
-            pass_on(vbuf, vsend, vrecv, t)
+        for t in range(chunks):
+            wait(bit(vbuf, t), vrecv.at[t])
+            pass_on(vbuf, vsend, vrecv, t, bit)
 
     def share_product(gy, put):
         for p in range(pieces):
@@ -319,9 +359,15 @@
             block = vbuf[tile] if piece == side else vbuf[tile, pl.ds(off, piece)]
             put(p, value + jnp.where(own, block.astype(jnp.float32), 0.0))
 
-    for n in range(1, floors + 1):
-        floor = lax.rem(z + n, floors)
-
+    far = []
+    for n in range(floors - 1):
+        down = floors - 1 - n
+        down = jnp.where(down <= z, down - 1, down)
+        up = jnp.where(n >= z, n + 1, n)
+        far.append(jnp.where(2 * z < floors, down, up))
+    order = far + [z]
+
+    def give2(floor):
         def put(p, value):
             p2send[floor, pl.ds(p * piece, piece)] = value.astype(p2send.dtype)
 
@@ -330,20 +376,24 @@
             p2send.at[floor], p2recv.at[floor], p2s.at[floor], p2r.at[floor], i, j + 1 - 2 * c
         ).start()
 
-    for n in range(1, floors + 1):
-        floor = lax.rem(z + n, floors)
-
+    def combine2(n, floor):
         def put(p, value):
             last[pl.ds(p * piece, piece)] = value
 
         share_product(2 * floor + c, put)
         wait(p2recv.at[floor], p2r.at[floor])
         last[...] += p2recv[floor].astype(jnp.float32)
-        if n < floors:
+        if n < floors - 1:
             r2send[floor] = last[...].astype(r2send.dtype)
             remote(
                 r2send.at[floor], r2recv.at[z], r2s.at[floor], r2r.at[z], i, 2 * floor + c
             ).start()
+
+    for n in range(floors + LAG2):
+        if n < floors:
+            give2(order[n])
+        if n >= LAG2:
+            combine2(n - LAG2, order[n - LAG2])
 
     for n in range(1, floors):
         floor = lax.rem(z + n, floors)
@@ -370,8 +420,8 @@
             lax.rem(other, blocks),
         ).start()
 
-    fan_done(sbuf, ssend)
-    fan_done(vbuf, vsend)
+    fan_done(sbuf, ssend, rows)
+    fan_done(vbuf, vsend, bit)
     for h in range(2):
         source = rs.at[pl.ds(h * col_tiles, col_tiles)]
         for n in range(groups):
@@ -390,8 +440,8 @@
 
     @pl.when(jnp.logical_not(root))
     def _():
-        for t in range(col_tiles):
-            wait(rows(csend, t), csd.at[t])
+        for t in range(chunks):
+            wait(bit(csend, t), csd.at[t])
 
     for n in range(1, floors + 1):
         floor = lax.rem(z + n, floors)
@@ -402,12 +452,16 @@
     others = sq.at[pl.ds(1, total - 1)]
     wait(others, qs)
     wait(others, qr)
-    sums = jnp.sum(sq[...], axis=0)
+    sums_out[...] = jnp.sum(sq[...], axis=0)
+    out[...] = last[...]
+
+
+def finish(nodes, mixed, sums, vectors, scales):
     first = jnp.sqrt(sums[0:1] / nodes + 1e-06)
     second = jnp.sqrt(sums[1:2] / (first * first) / nodes + 1e-06)
-    sums_out[0:1] = first
-    sums_out[1:2] = second
-    out[...] = last[...] / (first * second)
+    scales[0:1] = first
+    scales[1:2] = second
+    vectors[...] = (mixed[...] / (first * second)).astype(vectors.dtype)
 
 
 def on_device(groups, blocks, tiles, tile_cols, row_counts, start_block):
@@ -421,6 +475,7 @@
     floors = blocks // 2
     total = groups * blocks
     fan = 2 if groups == 4 else groups - 1
+    chunks = col_tiles * (2 if groups == 4 else 1)
     bf16, f32 = jnp.bfloat16, jnp.float32
     vmem, dma = pltpu.VMEM, pltpu.SemaphoreType.DMA
     spec = pl.BlockSpec
@@ -442,17 +497,17 @@
             vmem((col_tiles, side, width), bf16),
             vmem((col_tiles + 1, side, width), bf16),
             vmem((col_tiles + 1, side, width), bf16),
-            vmem((depth, width), f32),
+            vmem((col_tiles, side, width), f32),
             vmem((share_tiles * side, width), f32),
             vmem((row_tiles, 1, side), f32),
             vmem((blocks, col_tiles, 1, side), f32),
             vmem((blocks, share_tiles, 1, side), f32),
-            vmem((depth, width), bf16),
-            vmem((depth, width), bf16),
-            vmem((depth, width), f32),
-            vmem((depth, width), bf16),
-            vmem((depth, width), bf16),
-            vmem((depth, width), bf16),
+            vmem((col_tiles, side, width), bf16),
+            vmem((col_tiles, side, width), bf16),
+            vmem((col_tiles, side, width), f32),
+            vmem((col_tiles, side, width), bf16),
+            vmem((col_tiles, side, width), bf16),
+            vmem((col_tiles, side, width), bf16),
             vmem((floors, share, width), bf16),
             vmem((floors, share, width), bf16),
             vmem((floors, share, width), bf16),
@@ -468,21 +523,28 @@
             dma((blocks,)),
             dma((col_tiles,)),
             dma((col_tiles,)),
-            dma((col_tiles,)),
-            dma((col_tiles,)),
-            dma((col_tiles,)),
-            dma((fan, col_tiles)),
-            dma((col_tiles,)),
+            dma((chunks,)),
+            dma((chunks,)),
+            dma((chunks,)),
+            dma((fan, chunks)),
+            dma((chunks,)),
             dma((floors,)),
             dma((floors,)),
             dma((floors,)),
             dma((floors,)),
             dma,
             dma,
+            pltpu.SemaphoreType.REGULAR,
         ],
         compiler_params=pltpu.CompilerParams(collective_id=0, has_side_effects=True),
-    )(tiles, start_block, tile_cols, row_counts)
-    return out.astype(bf16), scales
+    )(tiles, start_block, tile_cols.T, row_counts.T)
+    return pl.pallas_call(
+        functools.partial(finish, local_rows * groups),
+        out_shape=(
+            jax.ShapeDtypeStruct((share, width), bf16),
+            jax.ShapeDtypeStruct((2, width), f32),
+        ),
+    )(out, scales)
 
 
 def solution(mesh):

time: 60 us -> 51.5 us (0.86)
  local copies, waits for them, and re-layouts: 3.9 us -> 0 us
  Pallas kernels: 53.6 us -> 50.7 us
  other arithmetic: 1.54 us -> 0 us
    pallas_call x1, Pallas kernels: 53.6 us -> 49.1 us  [on_device(): pl.pallas_call(functools.partial(kernel, groups, blocks), out_shape=(jax....]
    unnamed x3 -> x0, local copies, waits for them, and re-layouts: 3.9 us -> none
    pallas_call x0 -> x1, Pallas kernels: none -> 1.58 us  [on_device(): pl.pallas_call(functools.partial(finish, local_rows * groups), out_shape=...]
    convert_element_type x1 -> x0, other arithmetic: 1.54 us -> none  [on_device(): return (out.astype(bf16), scales)]
where the time goes in v2:
time: 51.5 us; the launch traced here: 51.3 us
  Pallas kernels  50.7 us (98%)
  between operations  0.64 us (1%)
    pallas_call x1, Pallas kernels, on_device(): pl.pallas_call(functools.partial(kernel, groups, blocks), out_shape=(jax....  49.1 us
    pallas_call x1, Pallas kernels, on_device(): pl.pallas_call(functools.partial(finish, local_rows * groups), out_shape=...  1.58 us

profile of v2, /device:TPU:0, one launch (start us, length us, event | category | flops | bytes accessed | tf_op | source)
XLA Modules:
  0.0 51.3 jit_solution(3121349126957867611)
XLA Ops:
  0.6 49.1 %shard_map.59 = (f32[256,128]{1,0:T(8,128)}, f32[2,128]{1,0:T(2,128)}) custom-call(bf16[16,3,128,128]{3,2,1,0:T(8,128)(2,1)} %tiles_hbm.1, bf16[2048,128]{1,0:T(8,128)(2,1)} %start_hbm.1, s32[3,16]{1,0:T(4,128)} %bitcast.2, s32[1,16]{1,0:T(1,128)} %bitcast.3), custom_call_target="tpu_custom_call" | custom-call | tf_op jit(solution)/shard_map/pallas_call | solution.py:482
  49.7 1.6 %shard_map.60 = (bf16[256,128]{1,0:T(8,128)(2,1)}, f32[2,128]{1,0:T(2,128)}) custom-call(f32[256,128]{1,0:T(8,128)} %get-tuple-element.4.mixed, f32[2,128]{1,0:T(2,128)} %get-tuple-element.5.sums), custom_call_target="tpu_custom_call" | custom-call | tf_op jit(solution)/shard_map/pallas_call | solution.py:541

commit v3 on v2

--- a/solution.py
+++ b/solution.py
@@ -8,7 +8,7 @@
 
 MESH = pl.DeviceIdType.MESH
 LOADS = 4
-LAG = 4
+LAG = 2
 LAG2 = 1
 
 
@@ -83,7 +83,6 @@
     j = lax.axis_index("gy")
     z = lax.div(j, 2)
     c = lax.rem(j, 2)
-    me = i * blocks + j
     root = i == z
     if square:
         x, y = lax.rem(i, 2), lax.div(i, 2)
@@ -408,17 +407,20 @@
     last[...] = mixed
     sq[0, 1:2] = jnp.sum(mixed * mixed, axis=0, keepdims=True)
 
-    @pl.loop(1, total)
-    def _(k):
-        other = lax.rem(me + k, total)
-        remote(
-            sq.at[0],
-            sq.at[total - k],
-            qs,
-            qr,
-            lax.div(other, blocks),
-            lax.rem(other, blocks),
-        ).start()
+    def tell(k, gx, gy):
+        remote(sq.at[0], sq.at[k], qs, qr, gx, gy).start()
+
+    if square:
+        across = [lax.rem(i + n, groups) for n in range(groups)]
+        along = [lax.rem(j + n, blocks) for n in range(blocks)]
+        for k in range(total - 1, 0, -1):
+            tell(k, across[k // blocks], along[k % blocks])
+    else:
+
+        @pl.loop(1, total)
+        def _(k):
+            gx, gy = lax.div(k, blocks), lax.rem(k, blocks)
+            tell(k, lax.rem(i + gx, groups), lax.rem(j + gy, blocks))
 
     fan_done(sbuf, ssend, rows)
     fan_done(vbuf, vsend, bit)

time: 51.5 us -> 51.5 us (level)
  no operation moved by 1% of the time
where the time goes in v3:
time: 51.5 us; the launch traced here: 51.4 us
  Pallas kernels  50.7 us (98%)
  between operations  0.64 us (1%)
    pallas_call x1, Pallas kernels, on_device(): pl.pallas_call(functools.partial(kernel, groups, blocks), out_shape=(jax....  49.1 us
    pallas_call x1, Pallas kernels, on_device(): pl.pallas_call(functools.partial(finish, local_rows * groups), out_shape=...  1.58 us

profile of v3, /device:TPU:0, one launch (start us, length us, event | category | flops | bytes accessed | tf_op | source)
XLA Modules:
  0.0 51.4 jit_solution(4861698724468631710)
XLA Ops:
  0.6 49.1 %shard_map.59 = (f32[256,128]{1,0:T(8,128)}, f32[2,128]{1,0:T(2,128)}) custom-call(bf16[16,3,128,128]{3,2,1,0:T(8,128)(2,1)} %tiles_hbm.1, bf16[2048,128]{1,0:T(8,128)(2,1)} %start_hbm.1, s32[3,16]{1,0:T(4,128)} %bitcast.2, s32[1,16]{1,0:T(1,128)} %bitcast.3), custom_call_target="tpu_custom_call" | custom-call | tf_op jit(solution)/shard_map/pallas_call | solution.py:484
  49.8 1.6 %shard_map.60 = (bf16[256,128]{1,0:T(8,128)(2,1)}, f32[2,128]{1,0:T(2,128)}) custom-call(f32[256,128]{1,0:T(8,128)} %get-tuple-element.4.mixed, f32[2,128]{1,0:T(2,128)} %get-tuple-element.5.sums), custom_call_target="tpu_custom_call" | custom-call | tf_op jit(solution)/shard_map/pallas_call | solution.py:543
